TPU v7x, 32 devices: a whole 2x2x4 slice. The times are simulated.
32 devices in a mesh: row: 8 (over z, core), col: 4 (over y, x).
Axes of the slice: x: 2, y: 2, z: 4, core: 2. Of those that a mesh axis runs over, the one named last changes fastest.
Arguments:
- tensor: bfloat16 [512, 2048, 256], P(('row', 'col')), may hold values from -6 to 6
- factor_one: bfloat16 [512, 64], P(('row', 'col')), may hold values from -0.25 to 0.25
- factor_two: bfloat16 [2048, 64], P('col'), may hold values from -0.125 to 0.125
Outputs:
- gram: float32 [256, 256], replicated
All inputs are finite; a program needn't handle non-finite values.
Results may differ from a plain program's by a relative error of at most 0.0003.
Values may be sent and summed in bfloat16 or wider, within the bound.
A program may use at most 64 MiB of HBM per device.

v0:
```python
import jax
import jax.numpy as jnp
from jax import lax
from jax.sharding import PartitionSpec as P

R1 = 64
R2 = 64


def apply_first(partly, first):
    return jnp.einsum(
        "ark,as->srk", partly, first.astype(jnp.float32), precision=lax.Precision.HIGHEST
    )


def per_device(tensor, factor_one, factor_two):
    whole_two = lax.all_gather(factor_two, "col", axis=0, tiled=True)
    partly = jnp.einsum("abk,br->ark", tensor, whole_two, preferred_element_type=jnp.float32)
    scale = R1 * R2
    partial_core = apply_first(partly, factor_one)
    flat_part = partial_core.reshape(R1 * R2, partial_core.shape[2])
    summed = lax.psum(flat_part, ("row", "col"))
    gram = jnp.dot(
        summed.T, summed, precision=lax.Precision.HIGHEST, preferred_element_type=jnp.float32
    )
    return gram / scale


def solution(mesh):
    placed = (P(("row", "col"), None, None), P(("row", "col"), None), P("col", None))
    return jax.shard_map(per_device, mesh=mesh, in_specs=placed, out_specs=P(), check_vma=False)
```

profile of v0, /device:TPU:0, one launch (start us, length us, event | category | flops | bytes accessed | tf_op | source)
XLA Modules:
  0.0 193.5 jit_solution(18068110036583877398)
XLA Ops:
  6.5 0.0 copy-start
  6.5 0.0 all-reduce.2.cloned.1.call-start
  6.5 10.9 %all_gather.3 = bf16[2048,64]{0,1:T(8,128)(2,1)S(1)} all-gather(bf16[512,64]{0,1:T(8,128)(2,1)} %param.5), channel_id=1, replica_groups=mesh['row'=8,'col'=4] {'col'}, dimensions={0}, use_global_device_ids=true | all-gather | bytes 327680 | tf_op jit(solution)/shard_map/all_gather | solution.py:17
  17.4 8.7 %fusion.2 = f32[64,16,256]{2,0,1:T(8,128)S(1)} fusion(bf16[16,2048,256]{2,1,0:T(8,128)(2,1)} %param.3, bf16[2048,64]{0,1:T(8,128)(2,1)S(1)} %all_gather.3), kind=kOutput, calls=%fused_computation.4 | convolution fusion | flops 1073741824 | bytes 18087936 | tf_op jit(solution)/shard_map/abk,br->ark/dot_general | solution.py:18
  26.2 0.0 copy-done
  26.2 2.1 %convolution_bitcast_fusion = f32[64,64,256]{2,0,1:T(8,128)S(1)} fusion(f32[64,16,256]{2,0,1:T(8,128)S(1)} %fusion.2, bf16[16,64]{1,0:T(8,128)(2,1)S(1)} %copy-done), kind=kOutput, calls=%fused_computation | convolution fusion | flops 201326592 | bytes 5244928 | tf_op jit(solution)/shard_map/ark,as->srk/dot_general | solution.py:11
  28.3 4.4 %copy.4 = f32[64,64,256]{2,1,0:T(8,128)} copy(f32[64,64,256]{2,0,1:T(8,128)S(1)} %convolution_bitcast_fusion) | data formatting | bytes 8388608 | tf_op jit(solution)/shard_map/ark,as->srk/dot_general | solution.py:11
  32.7 0.0 all-reduce.2.cloned.1.call-update
  32.7 143.0 %all-reduce.2.cloned.1.call-done = f32[4096,256]{1,0:T(8,128)} async-done(((f32[4096,256]{1,0:T(8,128)}), f32[4096,256]{1,0:T(8,128)}) %all-reduce.2.cloned.1.call-update) | async-done | bytes 4194320 | tf_op jit(solution)/shard_map/psum | solution.py:22
  175.7 10.9 %convolution_multiply_fusion = f32[256,256]{1,0:T(8,128)} fusion(f32[4096,256]{1,0:T(8,128)} %all-reduce.2.cloned.1.call-done), kind=kOutput, calls=%fused_computation.1 | convolution fusion | flops 3221291008 | bytes 4456448 | tf_op jit(solution)/shard_map/dot_general | solution.py:23
Async XLA Ops:
  6.5 19.6 %copy-start = (bf16[16,64]{1,0:T(8,128)(2,1)S(1)}, bf16[16,64]{1,0:T(8,128)(2,1)}, u32[]{:S(2)}) copy-start(bf16[16,64]{1,0:T(8,128)(2,1)} %param.4) | copy-start | bytes 6148
  6.5 169.2 %all-reduce.2.cloned.1.call-start = ((), (), s32[]{:S(2)}) async-start(), calls=%async_computation | async-start | bytes 8388608 | tf_op jit(solution)/shard_map/psum | solution.py:22
Sparse Core Ops, SparseCore 0:
  32.8 142.8 all-reduce.1
where the time goes:
time: 194 us; the launch traced here: 193 us
  waiting for transfers between devices  143 us (74%)
  matrix products  21.8 us (11%)
  between operations  13.4 us (7%)
  blocking collectives  10.9 us (6%)
  local copies, waits for them, and re-layouts  4.39 us (2%)
    psum x1, waiting for transfers between devices, per_device(): summed = lax.psum(flat_part, ('row', 'col'))  143 us
    dot_general x1, matrix products, per_device(): jnp.dot(summed.T, summed, precision=lax.Precision.HIGHEST, preferred_elem...  10.9 us
    all_gather x1, blocking collectives, per_device(): whole_two = lax.all_gather(factor_two, 'col', axis=0, tiled=True)  10.9 us
    dot_general x1, matrix products, per_device(): jnp.einsum('abk,br->ark', tensor, whole_two, preferred_element_type=jnp.f...  8.75 us
    dot_general x1, local copies, waits for them, and re-layouts, apply_first(): jnp.einsum('ark,as->srk', partly, first.astype(jnp.float32), precision=la...  4.39 us
  transfers between devices with their start and end apart: 1, of which 1 were waited for; matrix products, arithmetic and copies ran while one was open for 0% of the time, Pallas kernels for 0%

commit v1 on v0

--- a/solution.py
+++ b/solution.py
@@ -7,6 +7,24 @@
 R2 = 64
 
 
+def strings_lift(inputs, shard_in):
+    raw_out, tall, upper = (lax.axis_size("col"), lax.axis_index("col"), inputs.shape[0])
+    rack = [(k, (k + 1) % raw_out) for k in range(raw_out)]
+    ledger = [(k, (k - 1) % raw_out) for k in range(raw_out)]
+    v_next = raw_out // 2
+    clean = parts_out = inputs
+    main = shard_in(inputs, tall * upper)
+    kk = 1
+    while kk < v_next + 1:
+        clean = lax.ppermute(clean, axis_name="col", perm=rack)
+        if kk < raw_out - v_next:
+            parts_out = lax.ppermute(parts_out, "col", perm=ledger)
+            main = main + shard_in(parts_out, (tall + kk) % raw_out * upper)
+        main = main + shard_in(clean, (tall - kk) % raw_out * upper)
+        kk = kk + 1
+    return main
+
+
 def apply_first(partly, first):
     return jnp.einsum(
         "ark,as->srk", partly, first.astype(jnp.float32), precision=lax.Precision.HIGHEST
@@ -14,8 +32,15 @@
 
 
 def per_device(tensor, factor_one, factor_two):
-    whole_two = lax.all_gather(factor_two, "col", axis=0, tiled=True)
-    partly = jnp.einsum("abk,br->ark", tensor, whole_two, preferred_element_type=jnp.float32)
+    partly = strings_lift(
+        factor_two,
+        lambda part, at: jnp.einsum(
+            "abk,br->ark",
+            lax.dynamic_slice_in_dim(tensor, at, part.shape[0], axis=1),
+            part,
+            preferred_element_type=jnp.float32,
+        ),
+    )
     scale = R1 * R2
     partial_core = apply_first(partly, factor_one)
     flat_part = partial_core.reshape(R1 * R2, partial_core.shape[2])

time: 194 us -> 195 us (level)
  blocking collectives: 10.9 us -> 0 us
  matrix products: 21.8 us -> 28.1 us
  starting transfers between devices: 0.01 us -> 5.05 us
    all_gather x1 -> x0, blocking collectives: 10.9 us -> none  [per_device(): whole_two = lax.all_gather(factor_two, 'col', axis=0, tiled=True)]
    ppermute x0 -> x3, starting transfers between devices: none -> 5.04 us  [the longest x2 4.09 us: strings_lift(): clean = lax.ppermute(clean, axis_name='col', perm=rack)]
    dot_general x1 -> x4, matrix products: 8.75 us -> 12.2 us  [per_device(): jnp.einsum('abk,br->ark', lax.dynamic_slice_in_dim(tensor, at, part.shape...]
    dot_general x1, matrix products: 2.1 us -> 4.82 us  [apply_first(): jnp.einsum('ark,as->srk', partly, first.astype(jnp.float32), precision=la...]
  transfers between devices with their start and end apart: 1 -> 4, of which waited for: 1 -> 1; matrix products, arithmetic and copies ran while one was open for 0% -> 5% of each run, Pallas kernels for 0% -> 0%
where the time goes in v1:
time: 195 us
  waiting for transfers between devices  144 us (74%)
  matrix products  28.1 us (14%)
  between operations  13.5 us (7%)
  starting transfers between devices  5.05 us (3%)
  local copies, waits for them, and re-layouts  4.4 us (2%)
    psum x1, waiting for transfers between devices, per_device(): summed = lax.psum(flat_part, ('row', 'col'))  144 us
    dot_general x4, matrix products, per_device(): jnp.einsum('abk,br->ark', lax.dynamic_slice_in_dim(tensor, at, part.shape...  12.2 us
    dot_general x1, matrix products, per_device(): jnp.dot(summed.T, summed, precision=lax.Precision.HIGHEST, preferred_elem...  11.1 us
    dot_general x1, matrix products, apply_first(): jnp.einsum('ark,as->srk', partly, first.astype(jnp.float32), precision=la...  4.82 us
    dot_general x1, local copies, waits for them, and re-layouts, apply_first(): jnp.einsum('ark,as->srk', partly, first.astype(jnp.float32), precision=la...  4.39 us
    ppermute x2, starting transfers between devices, strings_lift(): clean = lax.ppermute(clean, axis_name='col', perm=rack)  4.09 us
  transfers between devices with their start and end apart: 4, of which 1 were waited for; matrix products, arithmetic and copies ran while one was open for 5% of the time, Pallas kernels for 0%

profile of v1, /device:TPU:0, one launch (start us, length us, event | category | flops | bytes accessed | tf_op | source)
XLA Modules:
  0.0 194.9 jit_solution(1353250398234768788)
XLA Ops:
  6.5 0.0 copy-start
  6.5 0.0 all-reduce.2.cloned.1.call-start
  6.5 3.0 %collective-permute-start.1 = (bf16[512,64]{0,1:T(8,128)(2,1)}, bf16[512,64]{0,1:T(8,128)(2,1)S(1)}, u32[]{:S(2)}, u32[]{:S(2)}) collective-permute-start(bf16[512,64]{0,1:T(8,128)(2,1)} %param.5), channel_id=1, source_target_pairs={{0,1},{1,2},{2,3},{3,0},{4,5},{5,6},{6,7},{7,4},{8,9},{9,10},{10,1... | collective-permute-start | bytes 196616 | tf_op jit(solution)/shard_map/ppermute | solution.py:19
  9.5 1.0 collective-permute-start
  10.5 3.1 %fusion.6 = f32[16,256,64]{1,2,0:T(8,128)S(1)} fusion(bf16[16,2048,256]{2,1,0:T(8,128)(2,1)} %param.3, s32[]{:T(128)S(6)} %select_n.27, bf16[512,64]{0,1:T(8,128)(2,1)} %param.5), kind=kOutput, calls=%fused_computation.6 | convolution fusion | flops 268435456 | bytes 5308420 | tf_op jit(solution)/shard_map/abk,br->ark/dot_general | solution.py:37
  13.6 0.0 collective-permute-done.1
  13.6 1.1 collective-permute-start.2
  14.7 3.0 %fusion.2 = f32[16,256,64]{1,2,0:T(8,128)S(1)} fusion(bf16[16,2048,256]{2,1,0:T(8,128)(2,1)} %param.3, s32[]{:T(128)S(6)} %select_n.31, bf16[512,64]{0,1:T(8,128)(2,1)S(1)} %collective-permute-done.1), kind=kOutput, calls=%fused_computation.2 | convolution fusion | flops 268435456 | bytes 5308420 | tf_op jit(solution)/shard_map/abk,br->ark/dot_general | solution.py:37
  17.8 0.0 collective-permute-done
  17.8 3.0 %fusion.4 = f32[16,256,64]{1,2,0:T(8,128)S(1)} fusion(bf16[16,2048,256]{2,1,0:T(8,128)(2,1)} %param.3, s32[]{:T(128)S(6)} %select_n.29, bf16[512,64]{0,1:T(8,128)(2,1)S(1)} %collective-permute-done), kind=kOutput, calls=%fused_computation.4 | convolution fusion | flops 268435456 | bytes 5308420 | tf_op jit(solution)/shard_map/abk,br->ark/dot_general | solution.py:37
  20.8 0.0 collective-permute-done.2
  20.8 3.0 %fusion = f32[16,256,64]{1,2,0:T(8,128)S(1)} fusion(bf16[16,2048,256]{2,1,0:T(8,128)(2,1)} %param.3, s32[]{:T(128)S(6)} %select_n.33, bf16[512,64]{0,1:T(8,128)(2,1)S(1)} %collective-permute-done.2), kind=kOutput, calls=%fused_computation | convolution fusion | flops 268435456 | bytes 5308420 | tf_op jit(solution)/shard_map/abk,br->ark/dot_general | solution.py:37
  23.9 0.0 copy-done
  23.9 4.8 %convolution_bitcast_fusion = f32[64,64,256]{2,0,1:T(8,128)S(1)} fusion(f32[16,256,64]{1,2,0:T(8,128)S(1)} %fusion, f32[16,256,64]{1,2,0:T(8,128)S(1)} %fusion.2, f32[16,256,64]{1,2,0:T(8,128)S(1)} %fusion.4, f32[16,256,64]{1,2,0:T(8,128)S(1)} %fusion.6, bf16[16,64]{1,0:T(8,128)(2,1)S(1)} %copy-done), kind=kOutput, calls=%fused_computation.8 | convolution fusion | flops 202113024 | bytes 8390656 | tf_op jit(solution)/shard_map/ark,as->srk/dot_general | solution.py:29
  28.7 4.4 %copy.4 = f32[64,64,256]{2,1,0:T(8,128)} copy(f32[64,64,256]{2,0,1:T(8,128)S(1)} %convolution_bitcast_fusion) | data formatting | bytes 8388608 | tf_op jit(solution)/shard_map/ark,as->srk/dot_general | solution.py:29
  33.1 0.0 all-reduce.2.cloned.1.call-update
  33.1 143.8 %all-reduce.2.cloned.1.call-done = f32[4096,256]{1,0:T(8,128)} async-done(((f32[4096,256]{1,0:T(8,128)}), f32[4096,256]{1,0:T(8,128)}) %all-reduce.2.cloned.1.call-update) | async-done | bytes 4194320 | tf_op jit(solution)/shard_map/psum | solution.py:47
  176.9 11.1 %convolution_multiply_fusion = f32[256,256]{1,0:T(8,128)} fusion(f32[4096,256]{1,0:T(8,128)} %all-reduce.2.cloned.1.call-done), kind=kOutput, calls=%fused_computation.9 | convolution fusion | flops 3221291008 | bytes 4456448 | tf_op jit(solution)/shard_map/dot_general | solution.py:48
Async XLA Ops:
  6.5 17.3 %copy-start = (bf16[16,64]{1,0:T(8,128)(2,1)S(1)}, bf16[16,64]{1,0:T(8,128)(2,1)}, u32[]{:S(2)}) copy-start(bf16[16,64]{1,0:T(8,128)(2,1)} %param.4) | copy-start | bytes 6148
  6.5 170.4 %all-reduce.2.cloned.1.call-start = ((), (), s32[]{:S(2)}) async-start(), calls=%async_computation | async-start | bytes 8388608 | tf_op jit(solution)/shard_map/psum | solution.py:47
  6.5 7.1 %collective-permute-start.1 = (bf16[512,64]{0,1:T(8,128)(2,1)}, bf16[512,64]{0,1:T(8,128)(2,1)S(1)}, u32[]{:S(2)}, u32[]{:S(2)}) collective-permute-start(bf16[512,64]{0,1:T(8,128)(2,1)} %param.5), channel_id=1, source_target_pairs={{0,1},{1,2},{2,3},{3,0},{4,5},{5,6},{6,7},{7,4},{8,9},{9,10},{10,1... | collective-permute-start | bytes 196616 | tf_op jit(solution)/shard_map/ppermute | solution.py:19
  9.5 8.3 %collective-permute-start = (bf16[512,64]{0,1:T(8,128)(2,1)}, bf16[512,64]{0,1:T(8,128)(2,1)S(1)}, u32[]{:S(2)}, u32[]{:S(2)}) collective-permute-start(bf16[512,64]{0,1:T(8,128)(2,1)} %param.5), channel_id=1, source_target_pairs={{0,3},{1,0},{2,1},{3,2},{4,7},{5,4},{6,5},{7,6},{8,11},{9,8},{10,9... | collective-permute-start | bytes 196616 | tf_op jit(solution)/shard_map/ppermute | solution.py:21
  13.6 7.2 %collective-permute-start.2 = (bf16[512,64]{0,1:T(8,128)(2,1)S(1)}, bf16[512,64]{0,1:T(8,128)(2,1)S(1)}, u32[]{:S(2)}, u32[]{:S(2)}) collective-permute-start(bf16[512,64]{0,1:T(8,128)(2,1)S(1)} %collective-permute-done.1), channel_id=1, source_target_pairs={{0,1},{1,2},{2,3},{3,0},{4,5},{5,6},{6,7},{7,4},{8,9},{9,10},{10,1... | collective-permute-start | bytes 196616 | tf_op jit(solution)/shard_map/ppermute | solution.py:19
Sparse Core Ops, SparseCore 0:
  33.2 143.6 all-reduce.1

commit v2 on v0

--- a/solution.py
+++ b/solution.py
@@ -7,6 +7,28 @@
 R2 = 64
 
 
+def see_types_here(local, shard_axis, dim_at):
+    amount_of = jax.lax.axis_size(shard_axis)
+    by_rank = []
+    for dev in range(amount_of):
+        by_rank.append((dev, (dev + 1) % amount_of))
+
+    def post_slices(u_next):
+        if len(u_next) == amount_of:
+            return u_next
+        val = post_slices(
+            [jax.lax.ppermute(u_next[0], axis_name=shard_axis, perm=by_rank), *u_next]
+        )
+        return val
+
+    ready = jnp.roll(
+        jnp.concatenate(post_slices([local]), axis=dim_at),
+        (jax.lax.axis_index(shard_axis) + 1) * local.shape[dim_at],
+        axis=dim_at,
+    )
+    return ready
+
+
 def apply_first(partly, first):
     return jnp.einsum(
         "ark,as->srk", partly, first.astype(jnp.float32), precision=lax.Precision.HIGHEST
@@ -14,7 +36,7 @@
 
 
 def per_device(tensor, factor_one, factor_two):
-    whole_two = lax.all_gather(factor_two, "col", axis=0, tiled=True)
+    whole_two = see_types_here(factor_two, "col", 0)
     partly = jnp.einsum("abk,br->ark", tensor, whole_two, preferred_element_type=jnp.float32)
     scale = R1 * R2
     partial_core = apply_first(partly, factor_one)

time: 194 us -> 202 us (1.041)
  waiting for transfers between devices: 143 us -> 156 us
  blocking collectives: 10.9 us -> 0 us
  starting transfers between devices: 0.01 us -> 4.24 us
    ppermute x0 -> x3, waiting for transfers between devices: none -> 12.5 us  [post_slices(): jax.lax.ppermute(u_next[0], axis_name=shard_axis, perm=by_rank)]
    all_gather x1 -> x0, blocking collectives: 10.9 us -> none  [per_device(): whole_two = lax.all_gather(factor_two, 'col', axis=0, tiled=True)]
    ppermute x0 -> x3, starting transfers between devices: none -> 4.23 us  [post_slices(): jax.lax.ppermute(u_next[0], axis_name=shard_axis, perm=by_rank)]
  transfers between devices with their start and end apart: 1 -> 4, of which waited for: 1 -> 4; matrix products, arithmetic and copies ran while one was open for 0% -> 0% of each run, Pallas kernels for 0% -> 0%
where the time goes in v2:
time: 202 us
  waiting for transfers between devices  156 us (77%)
  matrix products  21.8 us (11%)
  between operations  13.4 us (7%)
  local copies, waits for them, and re-layouts  6.13 us (3%)
  starting transfers between devices  4.24 us (2%)
    psum x1, waiting for transfers between devices, per_device(): summed = lax.psum(flat_part, ('row', 'col'))  143 us
    ppermute x3, waiting for transfers between devices, post_slices(): jax.lax.ppermute(u_next[0], axis_name=shard_axis, perm=by_rank)  12.5 us
    dot_general x1, matrix products, per_device(): jnp.dot(summed.T, summed, precision=lax.Precision.HIGHEST, preferred_elem...  10.9 us
    dot_general x1, matrix products, per_device(): jnp.einsum('abk,br->ark', tensor, whole_two, preferred_element_type=jnp.f...  8.75 us
    dot_general x1, local copies, waits for them, and re-layouts, apply_first(): jnp.einsum('ark,as->srk', partly, first.astype(jnp.float32), precision=la...  4.39 us
    ppermute x3, starting transfers between devices, post_slices(): jax.lax.ppermute(u_next[0], axis_name=shard_axis, perm=by_rank)  4.23 us
  transfers between devices with their start and end apart: 4, of which 4 were waited for; matrix products, arithmetic and copies ran while one was open for 0% of the time, Pallas kernels for 0%

profile of v2, /device:TPU:0, one launch (start us, length us, event | category | flops | bytes accessed | tf_op | source)
XLA Modules:
  0.0 201.5 jit_solution(16211037745078322438)
XLA Ops:
  6.5 0.0 copy-start
  6.5 0.0 all-reduce.2.cloned.1.call-start
  6.5 3.0 %collective-permute-start = (bf16[512,64]{0,1:T(8,128)(2,1)}, bf16[512,64]{0,1:T(8,128)(2,1)S(1)}, u32[]{:S(2)}, u32[]{:S(2)}) collective-permute-start(bf16[512,64]{0,1:T(8,128)(2,1)} %param.5), channel_id=1, source_target_pairs={{0,1},{1,2},{2,3},{3,0},{4,5},{5,6},{6,7},{7,4},{8,9},{9,10},{10,1... | collective-permute-start | bytes 196616 | tf_op jit(solution)/shard_map/ppermute | solution.py:20
  9.5 3.4 %collective-permute-done = bf16[512,64]{0,1:T(8,128)(2,1)S(1)} collective-permute-done((bf16[512,64]{0,1:T(8,128)(2,1)}, bf16[512,64]{0,1:T(8,128)(2,1)S(1)}, u32[]{:S(2)}, u32[]{:S(2)}) %collective-permute-start) | collective-permute-done | bytes 65568 | tf_op jit(solution)/shard_map/ppermute | solution.py:20
  12.9 1.1 collective-permute-start.1
  14.0 4.1 %collective-permute-done.1 = bf16[512,64]{0,1:T(8,128)(2,1)S(1)} collective-permute-done((bf16[512,64]{0,1:T(8,128)(2,1)S(1)}, bf16[512,64]{0,1:T(8,128)(2,1)S(1)}, u32[]{:S(2)}, u32[]{:S(2)}) %collective-permute-start.1) | collective-permute-done | bytes 65568 | tf_op jit(solution)/shard_map/ppermute | solution.py:20
  18.1 0.2 collective-permute-start.2
  18.3 5.0 %collective-permute-done.2 = bf16[512,64]{0,1:T(8,128)(2,1)S(1)} collective-permute-done((bf16[512,64]{0,1:T(8,128)(2,1)S(1)}, bf16[512,64]{0,1:T(8,128)(2,1)S(1)}, u32[]{:S(2)}, u32[]{:S(2)}) %collective-permute-start.2) | collective-permute-done | bytes 65568 | tf_op jit(solution)/shard_map/ppermute | solution.py:20
  23.3 0.8 constant_dynamic-update-slice_fusion.4
  24.2 0.8 constant_dynamic-update-slice_fusion
  25.0 8.7 %fusion.2 = f32[64,16,256]{2,0,1:T(8,128)S(1)} fusion(bf16[16,2048,256]{2,1,0:T(8,128)(2,1)} %param.3, bf16[4096,64]{0,1:T(8,128)(2,1)S(1)} %constant_dynamic-update-slice_fusion, s32[]{:T(128)S(6)} %select_n.14), kind=kOutput, calls=%fused_computation.4 | convolution fusion | flops 1073741824 | bytes 18087940 | tf_op jit(solution)/shard_map/abk,br->ark/dot_general | solution.py:40
  33.8 0.0 copy-done
  33.8 2.1 %convolution_bitcast_fusion = f32[64,64,256]{2,0,1:T(8,128)S(1)} fusion(f32[64,16,256]{2,0,1:T(8,128)S(1)} %fusion.2, bf16[16,64]{1,0:T(8,128)(2,1)S(1)} %copy-done), kind=kOutput, calls=%fused_computation | convolution fusion | flops 201326592 | bytes 5244928 | tf_op jit(solution)/shard_map/ark,as->srk/dot_general | solution.py:33
  35.9 4.4 %copy.4 = f32[64,64,256]{2,1,0:T(8,128)} copy(f32[64,64,256]{2,0,1:T(8,128)S(1)} %convolution_bitcast_fusion) | data formatting | bytes 8388608 | tf_op jit(solution)/shard_map/ark,as->srk/dot_general | solution.py:33
  40.3 0.0 all-reduce.2.cloned.1.call-update
  40.3 143.4 %all-reduce.2.cloned.1.call-done = f32[4096,256]{1,0:T(8,128)} async-done(((f32[4096,256]{1,0:T(8,128)}), f32[4096,256]{1,0:T(8,128)}) %all-reduce.2.cloned.1.call-update) | async-done | bytes 4194320 | tf_op jit(solution)/shard_map/psum | solution.py:44
  183.7 10.9 %convolution_multiply_fusion = f32[256,256]{1,0:T(8,128)} fusion(f32[4096,256]{1,0:T(8,128)} %all-reduce.2.cloned.1.call-done), kind=kOutput, calls=%fused_computation.1 | convolution fusion | flops 3221291008 | bytes 4456448 | tf_op jit(solution)/shard_map/dot_general | solution.py:45
  (6 shorter events, 0.0 us)
Async XLA Ops:
  6.5 27.2 %copy-start = (bf16[16,64]{1,0:T(8,128)(2,1)S(1)}, bf16[16,64]{1,0:T(8,128)(2,1)}, u32[]{:S(2)}) copy-start(bf16[16,64]{1,0:T(8,128)(2,1)} %param.4) | copy-start | bytes 6148
  6.5 177.2 %all-reduce.2.cloned.1.call-start = ((), (), s32[]{:S(2)}) async-start(), calls=%async_computation | async-start | bytes 8388608 | tf_op jit(solution)/shard_map/psum | solution.py:44
  6.5 6.4 %collective-permute-start = (bf16[512,64]{0,1:T(8,128)(2,1)}, bf16[512,64]{0,1:T(8,128)(2,1)S(1)}, u32[]{:S(2)}, u32[]{:S(2)}) collective-permute-start(bf16[512,64]{0,1:T(8,128)(2,1)} %param.5), channel_id=1, source_target_pairs={{0,1},{1,2},{2,3},{3,0},{4,5},{5,6},{6,7},{7,4},{8,9},{9,10},{10,1... | collective-permute-start | bytes 196616 | tf_op jit(solution)/shard_map/ppermute | solution.py:20
  12.9 5.2 %collective-permute-start.1 = (bf16[512,64]{0,1:T(8,128)(2,1)S(1)}, bf16[512,64]{0,1:T(8,128)(2,1)S(1)}, u32[]{:S(2)}, u32[]{:S(2)}) collective-permute-start(bf16[512,64]{0,1:T(8,128)(2,1)S(1)} %collective-permute-done), channel_id=1, source_target_pairs={{0,1},{1,2},{2,3},{3,0},{4,5},{5,6},{6,7},{7,4},{8,9},{9,10},{10,1... | collective-permute-start | bytes 196616 | tf_op jit(solution)/shard_map/ppermute | solution.py:20
  18.1 5.2 %collective-permute-start.2 = (bf16[512,64]{0,1:T(8,128)(2,1)S(1)}, bf16[512,64]{0,1:T(8,128)(2,1)S(1)}, u32[]{:S(2)}, u32[]{:S(2)}) collective-permute-start(bf16[512,64]{0,1:T(8,128)(2,1)S(1)} %collective-permute-done.1), channel_id=1, source_target_pairs={{0,1},{1,2},{2,3},{3,0},{4,5},{5,6},{6,7},{7,4},{8,9},{9,10},{10,1... | collective-permute-start | bytes 196616 | tf_op jit(solution)/shard_map/ppermute | solution.py:20
Sparse Core Ops, SparseCore 0:
  40.4 143.2 all-reduce.1

commit v3 on v0

--- a/solution.py
+++ b/solution.py
@@ -19,7 +19,9 @@
     scale = R1 * R2
     partial_core = apply_first(partly, factor_one)
     flat_part = partial_core.reshape(R1 * R2, partial_core.shape[2])
-    summed = lax.psum(flat_part, ("row", "col"))
+    summed = flat_part
+    for axis in ("col", "row"):
+        summed = lax.psum(summed, axis)
     gram = jnp.dot(
         summed.T, summed, precision=lax.Precision.HIGHEST, preferred_element_type=jnp.float32
     )

time: 194 us -> 254 us (1.31)
  waiting for transfers between devices: 143 us -> 203 us
    psum x1 -> x2, waiting for transfers between devices: 143 us -> 203 us  [per_device(): summed = lax.psum(summed, axis)]
  transfers between devices with their start and end apart: 1 -> 2, of which waited for: 1 -> 2; matrix products, arithmetic and copies ran while one was open for 0% -> 0% of each run, Pallas kernels for 0% -> 0%
where the time goes in v3:
time: 254 us; the launch traced here: 253 us
  waiting for transfers between devices  203 us (80%)
  matrix products  21.8 us (9%)
  between operations  13.4 us (5%)
  blocking collectives  10.9 us (4%)
  local copies, waits for them, and re-layouts  4.39 us (2%)
    psum x2, waiting for transfers between devices, per_device(): summed = lax.psum(summed, axis)  203 us
    dot_general x1, matrix products, per_device(): jnp.dot(summed.T, summed, precision=lax.Precision.HIGHEST, preferred_elem...  10.9 us
    all_gather x1, blocking collectives, per_device(): whole_two = lax.all_gather(factor_two, 'col', axis=0, tiled=True)  10.9 us
    dot_general x1, matrix products, per_device(): jnp.einsum('abk,br->ark', tensor, whole_two, preferred_element_type=jnp.f...  8.75 us
  transfers between devices with their start and end apart: 2, of which 2 were waited for; matrix products, arithmetic and copies ran while one was open for 0% of the time, Pallas kernels for 0%

profile of v3, /device:TPU:0, one launch (start us, length us, event | category | flops | bytes accessed | tf_op | source)
XLA Modules:
  0.0 253.4 jit_solution(12762084684466608124)
XLA Ops:
  6.5 0.0 copy-start
  6.5 0.0 all-reduce.3.cloned.1.call-start
  6.5 10.9 %all_gather.3 = bf16[2048,64]{0,1:T(8,128)(2,1)S(1)} all-gather(bf16[512,64]{0,1:T(8,128)(2,1)} %param.5), channel_id=1, replica_groups=mesh['row'=8,'col'=4] {'col'}, dimensions={0}, use_global_device_ids=true | all-gather | bytes 327680 | tf_op jit(solution)/shard_map/all_gather | solution.py:17
  17.4 8.7 %fusion.2 = f32[64,16,256]{2,0,1:T(8,128)S(1)} fusion(bf16[16,2048,256]{2,1,0:T(8,128)(2,1)} %param.3, bf16[2048,64]{0,1:T(8,128)(2,1)S(1)} %all_gather.3), kind=kOutput, calls=%fused_computation.4 | convolution fusion | flops 1073741824 | bytes 18087936 | tf_op jit(solution)/shard_map/abk,br->ark/dot_general | solution.py:18
  26.2 0.0 copy-done
  26.2 2.1 convolution_bitcast_fusion
  28.3 4.4 %copy.4 = f32[64,64,256]{2,1,0:T(8,128)} copy(f32[64,64,256]{2,0,1:T(8,128)S(1)} %convolution_bitcast_fusion) | data formatting | bytes 8388608 | tf_op jit(solution)/shard_map/ark,as->srk/dot_general | solution.py:11
  32.7 0.0 all-reduce.3.cloned.1.call-update
  32.7 0.2 all-reduce.5.cloned.1.call-start
  32.9 103.8 %all-reduce.3.cloned.1.call-done = f32[4096,256]{1,0:T(8,128)} async-done(((f32[4096,256]{1,0:T(8,128)}), f32[4096,256]{1,0:T(8,128)}) %all-reduce.3.cloned.1.call-update) | async-done | bytes 4194320 | tf_op jit(solution)/shard_map/psum | solution.py:24
  136.7 0.0 all-reduce.5.cloned.1.call-update
  136.7 98.9 %all-reduce.5.cloned.1.call-done = f32[4096,256]{1,0:T(8,128)} async-done(((f32[4096,256]{1,0:T(8,128)}), f32[4096,256]{1,0:T(8,128)}) %all-reduce.5.cloned.1.call-update) | async-done | bytes 4194320 | tf_op jit(solution)/shard_map/psum | solution.py:24
  235.6 10.9 %convolution_multiply_fusion = f32[256,256]{1,0:T(8,128)} fusion(f32[4096,256]{1,0:T(8,128)} %all-reduce.5.cloned.1.call-done), kind=kOutput, calls=%fused_computation.1 | convolution fusion | flops 3221291008 | bytes 4456448 | tf_op jit(solution)/shard_map/dot_general | solution.py:25
Async XLA Ops:
  6.5 19.6 %copy-start = (bf16[16,64]{1,0:T(8,128)(2,1)S(1)}, bf16[16,64]{1,0:T(8,128)(2,1)}, u32[]{:S(2)}) copy-start(bf16[16,64]{1,0:T(8,128)(2,1)} %param.4) | copy-start | bytes 6148
  6.5 130.2 %all-reduce.3.cloned.1.call-start = ((), (), s32[]{:S(2)}) async-start(), calls=%async_computation | async-start | bytes 8388608 | tf_op jit(solution)/shard_map/psum | solution.py:24
  32.7 202.9 %all-reduce.5.cloned.1.call-start = ((), (), s32[]{:S(2)}) async-start(), calls=%async_computation.1 | async-start | bytes 8388608 | tf_op jit(solution)/shard_map/psum | solution.py:24
Sparse Core Ops, SparseCore 0:
  32.8 103.8 all-reduce.2
  139.1 96.4 all-reduce.4
